TPU v7x, 32 devices: a whole 2x2x4 slice. The times are simulated.
32 devices in a mesh: ctx: 16 (over z, y, x), tp: 2 (over core).
Axes of the slice: x: 2, y: 2, z: 4, core: 2. Of those that a mesh axis runs over, the one named last changes fastest.
Arguments:
- byte_states: bfloat16 [4096, 1024], P('ctx'), may hold values from -12 to 12, as said below
- patch_of_byte: int32 [4096], P('ctx'), may hold values from 0 to 125, as said below
- patch_first: int32 [16], replicated, may hold values from 0 to 991, as said below
- moved: int32 [2, 16], replicated, may hold values from 0 to 32, as said below
- w_qkv: bfloat16 [3, 1024, 2048], P(None, None, 'tp'), may hold values from -0.25 to 0.25, as said below
- d_attn: bfloat16 [1024, 2048], P('ctx', 'tp'), may hold values from -6 to 6
Outputs:
- attn_out: bfloat16 [1024, 2048], P('ctx', 'tp')
- byte_grad: bfloat16 [4096, 1024], P('ctx', 'tp')
Inputs may be any that keep to these rules, and one draw needn't show every extreme that they name: `patch_of_byte`: within each byte shard the numbers start at 0 and rise by 0 or 1 from byte to byte; a shard holds at most 126 patches, reached on some shard. `patch_first`: the sum of the patch counts of all earlier byte shards; shard 0 starts at 0. moved[0, 0] = 0 and moved[1, 15] = 0; every other entry is 1 to 32; every patch shard thereby receives exactly 64 patches, and the patch counts agree with patch_first and patch_of_byte. `w_qkv`: independent entries of order 1024 ** -0.5. `byte_states`: entries of order one.
All inputs are finite; a program needn't handle non-finite values.
Results may differ from a plain program's by a relative error of at most 0.011.
Values may be sent and summed in bfloat16 or wider, within the bound.
A program may use at most 64 MiB of HBM per device.

v0:
```python
import jax
import jax.numpy as jnp
from jax import lax
from jax.sharding import PartitionSpec as P

HD = 128


def extended_2(x, sides, width):
    for axis, dim in sides:
        peers, length = (lax.axis_size(axis), x.shape[dim])
        up = [(i, (i + 1) % peers) for i in range(peers - 1)]
        down = [(j, i) for i, j in up]
        last = lax.slice_in_dim(x, length - width, length, axis=dim)
        first = lax.slice_in_dim(x, 0, width, axis=dim)
        before = lax.ppermute(last, axis, up)
        after = lax.ppermute(first, axis, down)
        x = jnp.concatenate([before, x, after], axis=dim)
    return x


def pick_own(values, index):
    return lax.dynamic_index_in_dim(values, index, 0, keepdims=False)


def shards(byte_states, patch_of_byte, patch_first, moved, w_qkv, d_attn):
    ctx_index = lax.axis_index("ctx")
    n_ctx = lax.axis_size("ctx")
    rows = d_attn.shape[0]
    feats = d_attn.shape[1]
    heads = feats // HD
    capacity = 2 * rows
    total = rows * n_ctx
    scale = HD ** (-0.5)
    ends = jnp.concatenate([patch_first[1:], jnp.full((1,), total, jnp.int32)])
    counts = ends - patch_first
    lower_moves = moved[0]
    upper_moves = moved[1]
    zero_one = jnp.zeros((1,), jnp.int32)
    below_high = jnp.concatenate([zero_one, upper_moves[:-1]])
    above_low = jnp.concatenate([lower_moves[1:], zero_one])
    prev_first = jnp.concatenate([zero_one, patch_first[:-1]])
    prev_count = jnp.concatenate([zero_one, counts[:-1]])
    ranks = jnp.arange(rows, dtype=jnp.int32)[None, :]
    from_low = ranks < below_high[:, None]
    from_high = ranks >= (rows - above_low)[:, None]
    lower_local = prev_count[:, None] - below_high[:, None] + ranks
    own_local = lower_moves[:, None] + ranks - below_high[:, None]
    upper_local = ranks - (rows - above_low)[:, None]
    ids_all = jnp.where(
        from_low,
        prev_first[:, None] + lower_local,
        jnp.where(from_high, ends[:, None] + upper_local, patch_first[:, None] + own_local),
    )
    source_all = jnp.where(
        from_low,
        lower_local,
        jnp.where(from_high, 2 * capacity + upper_local, capacity + own_local),
    )
    wanted = pick_own(ids_all, ctx_index)
    source_rows = pick_own(source_all, ctx_index)
    key_place = ids_all.reshape(-1)
    slots = jnp.arange(capacity, dtype=jnp.int32)
    member = patch_of_byte[None, :] == slots[:, None]
    lengths = jnp.sum(member.astype(jnp.float32), axis=1)
    onehot = member.astype(jnp.bfloat16)
    part = byte_states.shape[1] // lax.axis_size("tp")
    source = lax.dynamic_slice_in_dim(byte_states, lax.axis_index("tp") * part, part, 1)
    pooled_local = (
        jnp.dot(onehot, source, preferred_element_type=jnp.float32)
        / jnp.maximum(lengths, 1.0)[:, None]
    ).astype(jnp.bfloat16)
    extended = extended_2(pooled_local, (("ctx", 0),), capacity)
    picker = (source_rows[:, None] == jnp.arange(3 * capacity, dtype=jnp.int32)[None, :]).astype(
        jnp.bfloat16
    )
    pooled = jnp.dot(picker, extended, preferred_element_type=jnp.float32).astype(jnp.bfloat16)
    pooled = lax.all_gather(pooled, "tp", axis=1, tiled=True)
    query = jnp.dot(pooled, w_qkv[0], preferred_element_type=jnp.float32).astype(jnp.bfloat16)
    keyed = jnp.dot(pooled, w_qkv[1], preferred_element_type=jnp.float32).astype(jnp.bfloat16)
    valued = jnp.dot(pooled, w_qkv[2], preferred_element_type=jnp.float32).astype(jnp.bfloat16)
    keys_all, values_all = (
        lax.all_gather(keyed, "ctx", axis=0, tiled=True),
        lax.all_gather(valued, "ctx", axis=0, tiled=True),
    )
    query3 = query.reshape(rows, heads, HD)
    keys3 = keys_all.reshape(total, heads, HD)
    values3 = values_all.reshape(total, heads, HD)
    causal = (wanted[:, None] >= key_place[None, :])[None, :, :]
    score = jnp.einsum("qhd,khd->hqk", query3, keys3, preferred_element_type=jnp.float32) * scale
    masked = jnp.where(causal, score, -jnp.inf)
    top = jnp.max(masked, axis=2, keepdims=True)
    lse = top + jnp.log(jnp.sum(jnp.exp(masked - top), axis=2, keepdims=True))
    prob = jnp.exp(jnp.where(causal, score - lse, -jnp.inf))
    probs = prob.astype(jnp.bfloat16)
    output3 = jnp.einsum("hqk,khd->qhd", probs, values3, preferred_element_type=jnp.float32).astype(
        jnp.bfloat16
    )
    attn_out = output3.reshape(rows, feats)
    grad3 = d_attn.reshape(rows, heads, HD)
    delta = jnp.sum(grad3.astype(jnp.float32) * output3.astype(jnp.float32), axis=2)
    dprob = jnp.einsum("qhd,khd->hqk", grad3, values3, preferred_element_type=jnp.float32)
    dscore = (prob * (dprob - jnp.transpose(delta)[:, :, None])).astype(jnp.bfloat16)
    d_query = (
        jnp.einsum("hqk,khd->qhd", dscore, keys3, preferred_element_type=jnp.float32) * scale
    ).astype(jnp.bfloat16)
    lse_rows = jnp.transpose(lse[:, :, 0])
    lse_all, delta_all = (
        lax.all_gather(lse_rows, "ctx", axis=0, tiled=True),
        lax.all_gather(delta, "ctx", axis=0, tiled=True),
    )
    own_keys = keyed.reshape(rows, heads, HD)
    own_values = valued.reshape(rows, heads, HD)
    q_piece = lax.all_gather(query, "ctx", axis=0, tiled=True)
    g_piece = lax.all_gather(d_attn, "ctx", axis=0, tiled=True)
    count = q_piece.shape[0]
    q_three = q_piece.reshape(count, heads, HD)
    g_three = g_piece.reshape(count, heads, HD)
    lse_piece = jnp.transpose(lse_all)
    delta_piece = jnp.transpose(delta_all)
    allowed = (key_place[:, None] >= wanted[None, :])[None, :, :]
    part_score = (
        jnp.einsum("qhd,khd->hqk", q_three, own_keys, preferred_element_type=jnp.float32) * scale
    )
    part_prob = jnp.exp(jnp.where(allowed, part_score - lse_piece[:, :, None], -jnp.inf))
    part_probs = part_prob.astype(jnp.bfloat16)
    d_value_sum = jnp.einsum(
        "hqk,qhd->khd", part_probs, g_three, preferred_element_type=jnp.float32
    )
    part_dprob = jnp.einsum("qhd,khd->hqk", g_three, own_values, preferred_element_type=jnp.float32)
    part_dscore = (part_prob * (part_dprob - delta_piece[:, :, None])).astype(jnp.bfloat16)
    d_key_sum = (
        jnp.einsum("hqk,qhd->khd", part_dscore, q_three, preferred_element_type=jnp.float32) * scale
    )
    d_key_sum, d_value_sum = (d_key_sum, d_value_sum)
    d_key = d_key_sum.astype(jnp.bfloat16).reshape(rows, feats)
    d_value = d_value_sum.astype(jnp.bfloat16).reshape(rows, feats)
    d_query = d_query.reshape(rows, feats)
    contract = (((1,), (1,)), ((), ()))
    partial_value = lax.dot_general(d_query, w_qkv[0], contract, preferred_element_type=jnp.float32)
    partial_value = partial_value + lax.dot_general(
        d_key, w_qkv[1], contract, preferred_element_type=jnp.float32
    )
    partial_value = partial_value + lax.dot_general(
        d_value, w_qkv[2], contract, preferred_element_type=jnp.float32
    )
    d_pooled = lax.psum_scatter(partial_value, "tp", scatter_dimension=1, tiled=True).astype(
        jnp.bfloat16
    )
    returned = extended_2(d_pooled, (("ctx", 0),), rows)
    my_count = pick_own(counts, ctx_index)
    my_low = pick_own(lower_moves, ctx_index)
    my_high = pick_own(upper_moves, ctx_index)
    my_below = pick_own(below_high, ctx_index)
    target = jnp.where(
        patch_of_byte < my_low,
        rows - my_low + patch_of_byte,
        jnp.where(
            patch_of_byte >= my_count - my_high,
            2 * rows + patch_of_byte - (my_count - my_high),
            rows + my_below + patch_of_byte - my_low,
        ),
    )
    chooser = (target[:, None] == jnp.arange(3 * rows, dtype=jnp.int32)[None, :]).astype(
        jnp.bfloat16
    )
    spread_back = jnp.dot(chooser, returned, preferred_element_type=jnp.float32)
    byte_lengths = jnp.sum(jnp.where(member, lengths[:, None], 0.0), axis=0)
    byte_grad = (spread_back / byte_lengths[:, None]).astype(jnp.bfloat16)
    return (attn_out, byte_grad)


def solution(mesh):
    placed = (P("ctx", None), P("ctx"), P(), P(), P(None, None, "tp"), P("ctx", "tp"))
    return jax.shard_map(
        shards,
        mesh=mesh,
        in_specs=placed,
        out_specs=(P("ctx", "tp"), P("ctx", "tp")),
        check_vma=False,
    )
```

profile of v0, /device:TPU:6, one launch (start us, length us, event | category | flops | bytes accessed | tf_op | source)
XLA Modules:
  0.0 305.7 jit_solution(10949627991634043434)
XLA Ops:
  7.2 0.7 all-gather.13.cloned.1.call-update
  8.0 0.8 convert_reduce_fusion
  8.8 0.9 fusion.56
  9.7 3.4 %collective-permute-start = (bf16[128,512]{1,0:T(8,128)(2,1)S(1)}, bf16[128,512]{1,0:T(8,128)(2,1)S(1)}, u32[]{:S(2)}, u32[]{:S(2)}) collective-permute-start(bf16[128,512]{1,0:T(8,128)(2,1)S(1)} %fusion.56), channel_id=1, source_target_pairs={{0,2},{2,4},{4,6},{6,8},{8,10},{10,12},{12,14},{14,16},{16,18},{18... | collective-permute-start | bytes 393224 | tf_op jit(solution)/shard_map/ppermute | solution.py:16
  13.1 2.4 collective-permute-start.1
  15.5 0.8 slice_bitcast_fusion.1
  16.3 0.1 add_subtract_fusion.1
  16.4 0.8 fusion.133
  17.2 0.7 pad_add_fusion.3
  18.0 0.1 fusion.124
  18.0 0.8 fusion.132
  18.8 0.1 iota_compare_fusion.7
  19.0 0.1 add_subtract_fusion
  19.1 0.1 iota_compare_fusion.6
  19.2 1.2 dynamic-slice.3
  20.4 0.6 dynamic-slice.4
  21.0 0.6 dynamic-slice.2
  21.6 1.9 select_bitcast_fusion
  23.5 0.2 convolution_convert_fusion.1
  23.8 1.9 all_gather.21
  25.7 2.7 fusion.66
  28.5 2.7 fusion.60
  31.3 2.7 fusion.63
  34.2 0.1 lt.83
  34.3 0.1 add.195
  34.4 0.1 add.196
  34.9 0.1 ge.69
  35.0 0.1 add.201
  35.1 0.1 lt.82
  35.2 0.1 broadcast_compare_fusion.1
  35.3 0.1 broadcast_compare_fusion
  35.4 36.0 %all-gather.13.cloned.1.call-done = bf16[1024,1024]{1,0:T(8,128)(2,1)} async-done(((bf16[64,1024]{1,0:T(8,128)(2,1)}), bf16[1024,1024]{1,0:T(8,128)(2,1)}) %all-gather.13.cloned.1.call-update) | async-done | bytes 2097168 | tf_op jit(solution)/shard_map/all_gather | solution.py:115
  71.4 2.9 copy.61
  74.3 59.7 %all-gather.9.cloned.1.call-done = bf16[1024,1024]{1,0:T(8,128)(2,1)} async-done(((bf16[64,1024]{1,0:T(8,128)(2,1)}), bf16[1024,1024]{1,0:T(8,128)(2,1)}) %all-gather.9.cloned.1.call-update) | async-done | bytes 2097168 | tf_op jit(solution)/shard_map/all_gather | solution.py:83
  134.0 2.6 select_reduce_fusion
  136.6 1.3 copy-done.2
  137.9 0.6 exponential_reduce_fusion
  138.5 33.8 %all-gather = f32[16,64,8]{1,2,0:T(8,128)S(1)} all-gather(f32[1,64,8]{1,2,0:T(8,128)S(1)} %bitcast.202), channel_id=1, replica_groups=mesh['ctx'=16,'tp'=2] {'ctx'}, dimensions={0}, use_global_device_ids=true | all-gather | bytes 34816 | tf_op jit(solution)/shard_map/all_gather | solution.py:109
  172.3 0.1 reshape.379
  172.4 23.7 %all-gather.7.cloned.1.call-done = bf16[1024,1024]{1,0:T(8,128)(2,1)} async-done(((bf16[64,1024]{1,0:T(8,128)(2,1)}), bf16[1024,1024]{1,0:T(8,128)(2,1)}) %all-gather.7.cloned.1.call-update) | async-done | bytes 2097168 | tf_op jit(solution)/shard_map/all_gather | solution.py:84
  196.2 3.8 %multiply_reduce_fusion = (f32[64,8]{0,1:T(8,128)S(1)}, bf16[8,128,64]{1,2,0:T(8,128)(2,1)}) fusion(f32[8,64,1024]{2,1,0:T(8,128)} %copy-done.2, f32[8,64]{1,0:T(8,128)S(1)} %log_add_fusion, pred[64,1024]{1,0:T(8,128)(4,1)S(1)} %broadcast_compare_fusion.1, bf16[1024,1024]{1,0:T(8,128)(2,1)} %all-gather.7.cloned.1.call-done, bf16[64,1024]{1,0:T(8,128)(2,1)S(1)} %copy-done.6), kind=kOutput, calls=%fused_computation.75 | convolution fusion | flops 136642048 | bytes 4526080 | tf_op jit(solution)/shard_map/hqk,khd->qhd/dot_general | solution.py:96
  200.0 33.9 %all-gather.1 = f32[16,64,8]{1,2,0:T(8,128)S(1)} all-gather(f32[1,64,8]{1,2,0:T(8,128)S(1)} %bitcast.203), channel_id=1, replica_groups=mesh['ctx'=16,'tp'=2] {'ctx'}, dimensions={0}, use_global_device_ids=true | all-gather | bytes 34816 | tf_op jit(solution)/shard_map/all_gather | solution.py:110
  233.8 0.1 reshape.381
  233.9 24.8 %all-gather.11.cloned.1.call-done = bf16[1024,1024]{1,0:T(8,128)(2,1)} async-done(((bf16[64,1024]{1,0:T(8,128)(2,1)}), bf16[1024,1024]{1,0:T(8,128)(2,1)}) %all-gather.11.cloned.1.call-update) | async-done | bytes 2097168 | tf_op jit(solution)/shard_map/all_gather | solution.py:114
  258.7 2.7 select_exponential_fusion
  261.4 0.9 fusion.78
  262.3 0.5 copy-done.1
  262.8 3.3 %fusion.75 = bf16[8,8,8,128]{3,2,1,0:T(8,128)(2,1)S(1)} fusion(f32[8,1024,64]{1,2,0:T(8,128)} %copy-done.1, bf16[1024,8,128]{0,2,1:T(8,128)(2,1)S(1)} %bitcast.199, f32[8,1024]{1,0:T(8,128)S(1)} %bitcast.200, bf16[1024,1024]{1,0:T(8,128)(2,1)} %all-gather.11.cloned.1.call-done, bf16[64,1024]{1,0:T(8,128)(2,1)S(1)} %copy-done.4), kind=kOutput, calls=%fused_computation.60 | convolution fusion | flops 270139392 | bytes 6586368 | tf_op jit(solution)/shard_map/hqk,qhd->khd/dot_general | solution.py:133
  266.1 2.5 fusion.14
  268.6 4.0 %fusion.79 = bf16[8,8,8,128]{3,2,1,0:T(8,128)(2,1)S(1)} fusion(f32[8,64,1024]{2,1,0:T(8,128)S(1)} %copy-done.3, f32[8,64]{1,0:T(8,128)S(1)} %bitcast.204, f32[8,64]{1,0:T(8,128)S(1)} %log_add_fusion, pred[64,1024]{1,0:T(8,128)(4,1)S(1)} %broadcast_compare_fusion.1, bf16[1024,1024]{1,0:T(8,128)(2,1)} %all-gather.7.cloned.1.call-done, ...), kind=kOutput, calls=%fused_computation.62 | convolution fusion | flops 271712256 | bytes 6623232 | tf_op jit(solution)/shard_map/hqk,khd->qhd/dot_general | solution.py:105
  272.6 2.4 fusion.47
  275.0 3.1 %fusion.44 = f32[64,1024]{1,0:T(8,128)} fusion(f32[64,1024]{1,0:T(8,128)S(1)} %fusion.47, bf16[3,1024,1024]{2,1,0:T(8,128)(2,1)} %param.10, bf16[8,8,8,128]{3,2,1,0:T(8,128)(2,1)S(1)} %fusion.78), kind=kOutput, calls=%fused_computation.47 | convolution fusion | flops 134283264 | bytes 2752512 | tf_op jit(solution)/shard_map/dot_general | solution.py:144
  278.1 0.6 dynamic_slice.27
  278.7 0.6 dynamic_slice.29
  279.3 0.7 constant_dynamic-slice_fusion.3
  282.6 0.1 select_reduce_fusion.1
  282.7 0.7 compare_select_fusion.1
  283.4 2.6 reduce-scatter.2.cloned.1.call-done
  285.9 0.9 convert_element_type.89
  286.9 3.4 %collective-permute-start.2 = (bf16[64,512]{1,0:T(8,128)(2,1)S(1)}, bf16[64,512]{1,0:T(8,128)(2,1)S(1)}, u32[]{:S(2)}, u32[]{:S(2)}) collective-permute-start(bf16[64,512]{1,0:T(8,128)(2,1)S(1)} %convert_element_type.89), channel_id=1, source_target_pairs={{0,2},{2,4},{4,6},{6,8},{8,10},{10,12},{12,14},{14,16},{16,18},{18... | collective-permute-start | bytes 196616 | tf_op jit(solution)/shard_map/ppermute | solution.py:16
  290.2 2.5 collective-permute-start.3
  292.7 0.7 copy_bitcast_fusion
  293.4 4.8 %collective-permute-done.3 = bf16[64,512]{1,0:T(8,128)(2,1)S(1)} collective-permute-done((bf16[64,512]{1,0:T(8,128)(2,1)S(1)}, bf16[64,512]{1,0:T(8,128)(2,1)S(1)}, u32[]{:S(2)}, u32[]{:S(2)}) %collective-permute-start.3) | collective-permute-done | bytes 65568 | tf_op jit(solution)/shard_map/ppermute | solution.py:17
  298.2 1.0 fusion.43
  (49 shorter events, 1.2 us)
Async XLA Ops:
  7.2 1.6 copy-start
  7.2 64.3 %all-gather.13.cloned.1.call-start = ((), (), s32[]{:S(2)}) async-start(), calls=%async_computation.4 | async-start | bytes 2228224 | tf_op jit(solution)/shard_map/all_gather | solution.py:115
  7.9 126.1 %all-gather.9.cloned.1.call-start = ((), (), s32[]{:S(2)}) async-start(), calls=%async_computation.2 | async-start | bytes 2228224 | tf_op jit(solution)/shard_map/all_gather | solution.py:83
  9.7 13.9 %collective-permute-start = (bf16[128,512]{1,0:T(8,128)(2,1)S(1)}, bf16[128,512]{1,0:T(8,128)(2,1)S(1)}, u32[]{:S(2)}, u32[]{:S(2)}) collective-permute-start(bf16[128,512]{1,0:T(8,128)(2,1)S(1)} %fusion.56), channel_id=1, source_target_pairs={{0,2},{2,4},{4,6},{6,8},{8,10},{10,12},{12,14},{14,16},{16,18},{18... | collective-permute-start | bytes 393224 | tf_op jit(solution)/shard_map/ppermute | solution.py:16
  13.1 10.5 %collective-permute-start.1 = (bf16[128,512]{1,0:T(8,128)(2,1)S(1)}, bf16[128,512]{1,0:T(8,128)(2,1)S(1)}, u32[]{:S(2)}, u32[]{:S(2)}) collective-permute-start(bf16[128,512]{1,0:T(8,128)(2,1)S(1)} %fusion.56), channel_id=1, source_target_pairs={{2,0},{4,2},{6,4},{8,6},{10,8},{12,10},{14,12},{16,14},{18,16},{20... | collective-permute-start | bytes 393224 | tf_op jit(solution)/shard_map/ppermute | solution.py:17
  28.4 167.7 %all-gather.7.cloned.1.call-start = ((), (), s32[]{:S(2)}) async-start(), calls=%async_computation.1 | async-start | bytes 2228224 | tf_op jit(solution)/shard_map/all_gather | solution.py:84
  31.2 3.7 %copy-start.9 = (s32[16]{0:T(128)S(1)}, s32[16]{0:T(128)}, u32[]{:S(2)}) copy-start(s32[16]{0:T(128)} %param.8) | copy-start | bytes 196
  31.2 227.5 %all-gather.11.cloned.1.call-start = ((), (), s32[]{:S(2)}) async-start(), calls=%async_computation.3 | async-start | bytes 2228224 | tf_op jit(solution)/shard_map/all_gather | solution.py:114
  34.0 251.9 %reduce-scatter.2.cloned.1.call-start = ((), (), s32[]{:S(2)}) async-start(), calls=%async_computation.5 | async-start | bytes 393216 | tf_op jit(solution)/shard_map/reduce_scatter | solution.py:147
  35.4 98.6 %copy-start.5 = (bf16[64,1024]{1,0:T(8,128)(2,1)S(1)}, bf16[64,1024]{1,0:T(8,128)(2,1)}, u32[]{:S(2)}) copy-start(bf16[64,1024]{1,0:T(8,128)(2,1)} %fusion.63) | copy-start | bytes 393220
  136.6 1.4 copy-start.2
  136.6 59.6 %copy-start.6 = (bf16[64,1024]{1,0:T(8,128)(2,1)S(1)}, bf16[64,1024]{1,0:T(8,128)(2,1)}, u32[]{:S(2)}) copy-start(bf16[64,1024]{1,0:T(8,128)(2,1)} %param.11) | copy-start | bytes 393220
  172.4 86.3 %copy-start.7 = (bf16[64,1024]{1,0:T(8,128)(2,1)S(1)}, bf16[64,1024]{1,0:T(8,128)(2,1)}, u32[]{:S(2)}) copy-start(bf16[64,1024]{1,0:T(8,128)(2,1)} %fusion.66) | copy-start | bytes 393220
  261.4 1.4 copy-start.1
  261.4 1.4 copy-start.4
  266.1 2.5 copy-start.3
  275.0 7.6 %copy-start.10 = (s32[256]{0:T(256)S(1)}, s32[256]{0:T(256)}, u32[]{:S(2)}) copy-start(s32[256]{0:T(256)} %param.7) | copy-start | bytes 3076
  275.0 17.7 %copy-start.8 = (bf16[8,128,64]{1,2,0:T(8,128)(2,1)S(1)}, bf16[8,128,64]{1,2,0:T(8,128)(2,1)}, u32[]{:S(2)}) copy-start(bf16[8,128,64]{1,2,0:T(8,128)(2,1)} %get-tuple-element.18) | copy-start | bytes 393220
  286.9 6.5 %collective-permute-start.2 = (bf16[64,512]{1,0:T(8,128)(2,1)S(1)}, bf16[64,512]{1,0:T(8,128)(2,1)S(1)}, u32[]{:S(2)}, u32[]{:S(2)}) collective-permute-start(bf16[64,512]{1,0:T(8,128)(2,1)S(1)} %convert_element_type.89), channel_id=1, source_target_pairs={{0,2},{2,4},{4,6},{6,8},{8,10},{10,12},{12,14},{14,16},{16,18},{18... | collective-permute-start | bytes 196616 | tf_op jit(solution)/shard_map/ppermute | solution.py:16
  290.2 8.0 %collective-permute-start.3 = (bf16[64,512]{1,0:T(8,128)(2,1)S(1)}, bf16[64,512]{1,0:T(8,128)(2,1)S(1)}, u32[]{:S(2)}, u32[]{:S(2)}) collective-permute-start(bf16[64,512]{1,0:T(8,128)(2,1)S(1)} %convert_element_type.89), channel_id=1, source_target_pairs={{2,0},{4,2},{6,4},{8,6},{10,8},{12,10},{14,12},{16,14},{18,16},{20... | collective-permute-start | bytes 196616 | tf_op jit(solution)/shard_map/ppermute | solution.py:17
Sparse Core Ops, SparseCore 0:
  10.8 60.6 all-gather.12
  74.8 59.1 all-gather.8
  136.8 59.3 all-gather.6
  199.4 59.2 all-gather.10
  278.3 7.6 reduce-scatter.1
where the time goes:
time: 306 us
  waiting for transfers between devices  152 us (50%)
  blocking collectives  69.5 us (23%)
  matrix products  35.5 us (12%)
  between operations  16.7 us (5%)
  local copies, waits for them, and re-layouts  13.3 us (4%)
  starting transfers between devices  11.9 us (4%)
  other arithmetic  6.49 us (2%)
    all_gather x1, waiting for transfers between devices, shards(): lax.all_gather(keyed, 'ctx', axis=0, tiled=True)  59.7 us
    all_gather x1, waiting for transfers between devices, shards(): g_piece = lax.all_gather(d_attn, 'ctx', axis=0, tiled=True)  36 us
    all_gather x1, blocking collectives, shards(): lax.all_gather(delta, 'ctx', axis=0, tiled=True)  33.9 us
    all_gather x1, blocking collectives, shards(): lax.all_gather(lse_rows, 'ctx', axis=0, tiled=True)  33.8 us
    all_gather x1, waiting for transfers between devices, shards(): q_piece = lax.all_gather(query, 'ctx', axis=0, tiled=True)  24.8 us
    all_gather x1, waiting for transfers between devices, shards(): lax.all_gather(valued, 'ctx', axis=0, tiled=True)  23.7 us
    ppermute x2, starting transfers between devices, extended_2(): before = lax.ppermute(last, axis, up)  6.77 us
  transfers between devices with their start and end apart: 9, of which 6 were waited for; matrix products, arithmetic and copies ran while one was open for 11% of the time, Pallas kernels for 0%

commit v1 on v0

--- a/solution.py
+++ b/solution.py
@@ -112,7 +112,15 @@
     own_keys = keyed.reshape(rows, heads, HD)
     own_values = valued.reshape(rows, heads, HD)
     q_piece = lax.all_gather(query, "ctx", axis=0, tiled=True)
-    g_piece = lax.all_gather(d_attn, "ctx", axis=0, tiled=True)
+    g_piece = jnp.concatenate(
+        lax.all_to_all(
+            jnp.stack([d_attn for _ in range(lax.axis_size("ctx"))]),
+            "ctx",
+            concat_axis=0,
+            split_axis=0,
+        ),
+        axis=0,
+    )
     count = q_piece.shape[0]
     q_three = q_piece.reshape(count, heads, HD)
     g_three = g_piece.reshape(count, heads, HD)

time: 306 us -> 281 us (0.918)
  waiting for transfers between devices: 152 us -> 117 us
  starting transfers between devices: 11.9 us -> 19.1 us
    all_to_all x0 -> x1, waiting for transfers between devices: none -> 46.8 us  [shards(): lax.all_to_all(jnp.stack([d_attn for _ in range(lax.axis_size('ctx'))]),...]
    all_gather x1, waiting for transfers between devices: 59.7 us -> 14.2 us  [shards(): lax.all_gather(keyed, 'ctx', axis=0, tiled=True)]
    all_gather x1 -> x0, waiting for transfers between devices: 36 us -> none  [shards(): g_piece = lax.all_gather(d_attn, 'ctx', axis=0, tiled=True)]
    all_to_all x0 -> x1, starting transfers between devices: none -> 7.25 us  [shards(): lax.all_to_all(jnp.stack([d_attn for _ in range(lax.axis_size('ctx'))]),...]
    unnamed x24 -> x27, local copies, waits for them, and re-layouts: 2.04 us -> 5.88 us
  transfers between devices with their start and end apart: 9 -> 9, of which waited for: 6 -> 6; matrix products, arithmetic and copies ran while one was open for 11% -> 10% of each run, Pallas kernels for 0% -> 0%
where the time goes in v1:
time: 281 us
  waiting for transfers between devices  117 us (42%)
  blocking collectives  70.1 us (25%)
  matrix products  35.8 us (13%)
  starting transfers between devices  19.1 us (7%)
  between operations  16.6 us (6%)
  local copies, waits for them, and re-layouts  16 us (6%)
  other arithmetic  6.54 us (2%)
    all_to_all x1, waiting for transfers between devices, shards(): lax.all_to_all(jnp.stack([d_attn for _ in range(lax.axis_size('ctx'))]),...  46.8 us
    all_gather x1, blocking collectives, shards(): lax.all_gather(lse_rows, 'ctx', axis=0, tiled=True)  34.1 us
    all_gather x1, blocking collectives, shards(): lax.all_gather(delta, 'ctx', axis=0, tiled=True)  34 us
    all_gather x1, waiting for transfers between devices, shards(): q_piece = lax.all_gather(query, 'ctx', axis=0, tiled=True)  24.7 us
    all_gather x1, waiting for transfers between devices, shards(): lax.all_gather(valued, 'ctx', axis=0, tiled=True)  23.4 us
    all_gather x1, waiting for transfers between devices, shards(): lax.all_gather(keyed, 'ctx', axis=0, tiled=True)  14.2 us
    all_to_all x1, starting transfers between devices, shards(): lax.all_to_all(jnp.stack([d_attn for _ in range(lax.axis_size('ctx'))]),...  7.25 us
    ppermute x2, starting transfers between devices, extended_2(): before = lax.ppermute(last, axis, up)  6.77 us
  transfers between devices with their start and end apart: 9, of which 6 were waited for; matrix products, arithmetic and copies ran while one was open for 10% of the time, Pallas kernels for 0%

profile of v1, /device:TPU:6, one launch (start us, length us, event | category | flops | bytes accessed | tf_op | source)
XLA Modules:
  0.0 280.7 jit_solution(2057146116143918981)
XLA Ops:
  7.2 0.8 convert_reduce_fusion
  8.1 0.2 copy-done
  8.2 0.9 fusion.71
  9.1 3.4 %collective-permute-start = (bf16[128,512]{1,0:T(8,128)(2,1)S(1)}, bf16[128,512]{1,0:T(8,128)(2,1)S(1)}, u32[]{:S(2)}, u32[]{:S(2)}) collective-permute-start(bf16[128,512]{1,0:T(8,128)(2,1)S(1)} %fusion.71), channel_id=1, source_target_pairs={{0,2},{2,4},{4,6},{6,8},{8,10},{10,12},{12,14},{14,16},{16,18},{18... | collective-permute-start | bytes 393224 | tf_op jit(solution)/shard_map/ppermute | solution.py:16
  12.5 2.4 collective-permute-start.1
  15.0 0.8 slice_bitcast_fusion.1
  15.8 0.8 fusion.151
  16.5 0.8 fusion.152
  17.3 0.7 pad_add_fusion.3
  18.1 0.1 fusion.143
  18.2 0.1 iota_compare_fusion.7
  18.4 0.1 add_subtract_fusion.1
  18.5 0.1 iota_subtract_fusion
  18.5 0.1 iota_compare_fusion.6
  18.6 1.2 dynamic-slice.3
  19.9 0.6 dynamic-slice.4
  20.4 0.6 dynamic-slice.2
  21.0 1.9 select_bitcast_fusion
  23.0 0.2 convolution_convert_fusion
  23.2 1.9 all_gather.18
  25.1 2.8 fusion.81
  28.0 2.7 fusion.75
  30.7 1.6 stack.2
  32.3 7.3 %all-to-all-start = ((bf16[16,64,1024]{2,1,0:T(8,128)(2,1)}), bf16[16,64,1024]{2,1,0:T(8,128)(2,1)S(1)}, u32[]{:S(2)}, u32[]{:S(2)}) async-start(bf16[16,64,1024]{2,1,0:T(8,128)(2,1)} %stack.2), calls=%async_computation | async-start | bytes 4194304 | tf_op jit(solution)/shard_map/all_to_all | solution.py:116
  39.7 2.7 fusion.78
  43.0 0.1 add.199
  43.1 0.1 add.202
  43.2 0.1 ge.69
  43.6 0.1 broadcast_compare_fusion.1
  43.7 0.1 broadcast_compare_fusion
  43.8 46.8 %all-to-all-done = bf16[16,64,1024]{2,1,0:T(8,128)(2,1)S(1)} async-done(((bf16[16,64,1024]{2,1,0:T(8,128)(2,1)}), bf16[16,64,1024]{2,1,0:T(8,128)(2,1)S(1)}, u32[]{:S(2)}, u32[]{:S(2)}) %all-to-all-start) | async-done | bytes 2097184 | tf_op jit(solution)/shard_map/all_to_all | solution.py:116
  90.5 1.4 copy-done.4
  91.9 2.2 copy.77
  94.2 14.2 %all-gather.8.cloned.1.call-done = bf16[1024,1024]{1,0:T(8,128)(2,1)} async-done(((bf16[64,1024]{1,0:T(8,128)(2,1)}), bf16[1024,1024]{1,0:T(8,128)(2,1)}) %all-gather.8.cloned.1.call-update) | async-done | bytes 2097168 | tf_op jit(solution)/shard_map/all_gather | solution.py:83
  108.3 2.6 select_reduce_fusion
  110.9 1.4 copy-done.2
  112.3 0.6 exponential_reduce_fusion
  112.9 34.1 %all-gather = f32[16,64,8]{1,2,0:T(8,128)S(1)} all-gather(f32[1,64,8]{1,2,0:T(8,128)S(1)} %bitcast.203), channel_id=1, replica_groups=mesh['ctx'=16,'tp'=2] {'ctx'}, dimensions={0}, use_global_device_ids=true | all-gather | bytes 34816 | tf_op jit(solution)/shard_map/all_gather | solution.py:109
  147.0 0.1 reshape.377
  147.1 23.4 %all-gather.6.cloned.1.call-done = bf16[1024,1024]{1,0:T(8,128)(2,1)} async-done(((bf16[64,1024]{1,0:T(8,128)(2,1)}), bf16[1024,1024]{1,0:T(8,128)(2,1)}) %all-gather.6.cloned.1.call-update) | async-done | bytes 2097168 | tf_op jit(solution)/shard_map/all_gather | solution.py:84
  170.6 3.8 %multiply_reduce_fusion = (f32[64,8]{0,1:T(8,128)S(1)}, bf16[8,128,64]{1,2,0:T(8,128)(2,1)}) fusion(f32[8,64,1024]{2,1,0:T(8,128)} %copy-done.2, f32[8,64]{1,0:T(8,128)S(1)} %log_add_fusion, pred[64,1024]{1,0:T(8,128)(4,1)S(1)} %broadcast_compare_fusion.1, bf16[1024,1024]{1,0:T(8,128)(2,1)} %all-gather.6.cloned.1.call-done, bf16[64,1024]{1,0:T(8,128)(2,1)S(1)} %copy-done.7), kind=kOutput, calls=%fused_computation.79 | convolution fusion | flops 136642048 | bytes 4526080 | tf_op jit(solution)/shard_map/hqk,khd->qhd/dot_general | solution.py:96
  174.4 34.0 %all-gather.1 = f32[16,64,8]{1,2,0:T(8,128)S(1)} all-gather(f32[1,64,8]{1,2,0:T(8,128)S(1)} %bitcast.204), channel_id=1, replica_groups=mesh['ctx'=16,'tp'=2] {'ctx'}, dimensions={0}, use_global_device_ids=true | all-gather | bytes 34816 | tf_op jit(solution)/shard_map/all_gather | solution.py:110
  208.4 0.1 reshape.379
  208.5 24.7 %all-gather.10.cloned.1.call-done = bf16[1024,1024]{1,0:T(8,128)(2,1)} async-done(((bf16[64,1024]{1,0:T(8,128)(2,1)}), bf16[1024,1024]{1,0:T(8,128)(2,1)}) %all-gather.10.cloned.1.call-update) | async-done | bytes 2097168 | tf_op jit(solution)/shard_map/all_gather | solution.py:114
  233.2 2.7 select_exponential_fusion
  235.9 0.8 fusion.95
  236.8 0.6 copy-done.1
  237.3 3.7 %fusion.90 = bf16[8,8,8,128]{3,2,1,0:T(8,128)(2,1)S(1)} fusion(f32[8,1024,64]{1,2,0:T(8,128)} %copy-done.1, bf16[1024,8,128]{2,1,0:T(8,128)(2,1)S(1)} %bitcast.199, f32[8,1024]{1,0:T(8,128)S(1)} %bitcast.201, bf16[1024,1024]{1,0:T(8,128)(2,1)} %all-gather.10.cloned.1.call-done, bf16[64,1024]{1,0:T(8,128)(2,1)S(1)} %copy-done.5), kind=kOutput, calls=%fused_computation.64 | convolution fusion | flops 270139392 | bytes 6586368 | tf_op jit(solution)/shard_map/hqk,qhd->khd/dot_general | solution.py:141
  241.1 2.5 fusion.14
  243.6 4.0 %fusion.98 = bf16[8,8,8,128]{3,2,1,0:T(8,128)(2,1)S(1)} fusion(f32[8,64,1024]{2,1,0:T(8,128)S(1)} %copy-done.3, f32[8,64]{1,0:T(8,128)S(1)} %bitcast.205, f32[8,64]{1,0:T(8,128)S(1)} %log_add_fusion, pred[64,1024]{1,0:T(8,128)(4,1)S(1)} %broadcast_compare_fusion.1, bf16[1024,1024]{1,0:T(8,128)(2,1)} %all-gather.6.cloned.1.call-done, ...), kind=kOutput, calls=%fused_computation.66 | convolution fusion | flops 271712256 | bytes 6623232 | tf_op jit(solution)/shard_map/hqk,khd->qhd/dot_general | solution.py:105
  247.6 2.4 fusion.55
  250.0 3.1 %fusion.52 = f32[64,1024]{1,0:T(8,128)} fusion(f32[64,1024]{1,0:T(8,128)S(1)} %fusion.55, bf16[3,1024,1024]{2,1,0:T(8,128)(2,1)} %param.10, bf16[8,8,8,128]{3,2,1,0:T(8,128)(2,1)S(1)} %fusion.95), kind=kOutput, calls=%fused_computation.51 | convolution fusion | flops 134283264 | bytes 2752512 | tf_op jit(solution)/shard_map/dot_general | solution.py:152
  253.1 0.6 dynamic_slice.27
  253.7 0.6 dynamic_slice.29
  254.3 0.7 constant_dynamic-slice_fusion.3
  257.5 0.1 select_reduce_fusion.1
  257.6 0.7 compare_select_fusion.1
  258.3 2.6 reduce-scatter.2.cloned.1.call-done
  260.9 0.9 convert_element_type.89
  261.8 3.4 %collective-permute-start.2 = (bf16[64,512]{1,0:T(8,128)(2,1)S(1)}, bf16[64,512]{1,0:T(8,128)(2,1)S(1)}, u32[]{:S(2)}, u32[]{:S(2)}) collective-permute-start(bf16[64,512]{1,0:T(8,128)(2,1)S(1)} %convert_element_type.89), channel_id=1, source_target_pairs={{0,2},{2,4},{4,6},{6,8},{8,10},{10,12},{12,14},{14,16},{16,18},{18... | collective-permute-start | bytes 196616 | tf_op jit(solution)/shard_map/ppermute | solution.py:16
  265.2 2.5 collective-permute-start.3
  267.7 0.7 copy_bitcast_fusion
  268.4 4.8 %collective-permute-done.3 = bf16[64,512]{1,0:T(8,128)(2,1)S(1)} collective-permute-done((bf16[64,512]{1,0:T(8,128)(2,1)S(1)}, bf16[64,512]{1,0:T(8,128)(2,1)S(1)}, u32[]{:S(2)}, u32[]{:S(2)}) %collective-permute-start.3) | collective-permute-done | bytes 65568 | tf_op jit(solution)/shard_map/ppermute | solution.py:17
  273.1 1.0 fusion.51
  (51 shorter events, 1.3 us)
Async XLA Ops:
  7.2 1.1 copy-start
  7.2 101.1 %all-gather.8.cloned.1.call-start = ((), (), s32[]{:S(2)}) async-start(), calls=%async_computation.3 | async-start | bytes 2228224 | tf_op jit(solution)/shard_map/all_gather | solution.py:83
  9.1 13.9 %collective-permute-start = (bf16[128,512]{1,0:T(8,128)(2,1)S(1)}, bf16[128,512]{1,0:T(8,128)(2,1)S(1)}, u32[]{:S(2)}, u32[]{:S(2)}) collective-permute-start(bf16[128,512]{1,0:T(8,128)(2,1)S(1)} %fusion.71), channel_id=1, source_target_pairs={{0,2},{2,4},{4,6},{6,8},{8,10},{10,12},{12,14},{14,16},{16,18},{18... | collective-permute-start | bytes 393224 | tf_op jit(solution)/shard_map/ppermute | solution.py:16
  12.5 10.5 %collective-permute-start.1 = (bf16[128,512]{1,0:T(8,128)(2,1)S(1)}, bf16[128,512]{1,0:T(8,128)(2,1)S(1)}, u32[]{:S(2)}, u32[]{:S(2)}) collective-permute-start(bf16[128,512]{1,0:T(8,128)(2,1)S(1)} %fusion.71), channel_id=1, source_target_pairs={{2,0},{4,2},{6,4},{8,6},{10,8},{12,10},{14,12},{16,14},{18,16},{20... | collective-permute-start | bytes 393224 | tf_op jit(solution)/shard_map/ppermute | solution.py:17
  25.1 5.6 %copy-start.7 = (bf16[64,1024]{1,0:T(8,128)(2,1)S(1)}, bf16[64,1024]{1,0:T(8,128)(2,1)}, u32[]{:S(2)}) copy-start(bf16[64,1024]{1,0:T(8,128)(2,1)} %param.11) | copy-start | bytes 393220
  27.9 142.6 %all-gather.6.cloned.1.call-start = ((), (), s32[]{:S(2)}) async-start(), calls=%async_computation.2 | async-start | bytes 2228224 | tf_op jit(solution)/shard_map/all_gather | solution.py:84
  32.3 58.2 %all-to-all-start = ((bf16[16,64,1024]{2,1,0:T(8,128)(2,1)}), bf16[16,64,1024]{2,1,0:T(8,128)(2,1)S(1)}, u32[]{:S(2)}, u32[]{:S(2)}) async-start(bf16[16,64,1024]{2,1,0:T(8,128)(2,1)} %stack.2), calls=%async_computation | async-start | bytes 4194304 | tf_op jit(solution)/shard_map/all_to_all | solution.py:116
  39.6 3.7 %copy-start.10 = (s32[16]{0:T(128)S(1)}, s32[16]{0:T(128)}, u32[]{:S(2)}) copy-start(s32[16]{0:T(128)} %param.8) | copy-start | bytes 196
  39.6 193.6 %all-gather.10.cloned.1.call-start = ((), (), s32[]{:S(2)}) async-start(), calls=%async_computation.4 | async-start | bytes 2228224 | tf_op jit(solution)/shard_map/all_gather | solution.py:114
  42.4 218.5 %reduce-scatter.2.cloned.1.call-start = ((), (), s32[]{:S(2)}) async-start(), calls=%async_computation.5 | async-start | bytes 393216 | tf_op jit(solution)/shard_map/reduce_scatter | solution.py:155
  90.5 1.4 copy-start.4
  91.9 16.4 %copy-start.6 = (bf16[64,1024]{1,0:T(8,128)(2,1)S(1)}, bf16[64,1024]{1,0:T(8,128)(2,1)}, u32[]{:S(2)}) copy-start(bf16[64,1024]{1,0:T(8,128)(2,1)} %fusion.78) | copy-start | bytes 393220
  110.9 1.4 copy-start.2
  147.1 86.1 %copy-start.8 = (bf16[64,1024]{1,0:T(8,128)(2,1)S(1)}, bf16[64,1024]{1,0:T(8,128)(2,1)}, u32[]{:S(2)}) copy-start(bf16[64,1024]{1,0:T(8,128)(2,1)} %fusion.81) | copy-start | bytes 393220
  235.9 1.4 copy-start.1
  235.9 1.4 copy-start.5
  241.1 2.5 copy-start.3
  249.9 7.6 %copy-start.11 = (s32[256]{0:T(256)S(1)}, s32[256]{0:T(256)}, u32[]{:S(2)}) copy-start(s32[256]{0:T(256)} %param.7) | copy-start | bytes 3076
  249.9 17.7 %copy-start.9 = (bf16[8,128,64]{1,2,0:T(8,128)(2,1)S(1)}, bf16[8,128,64]{1,2,0:T(8,128)(2,1)}, u32[]{:S(2)}) copy-start(bf16[8,128,64]{1,2,0:T(8,128)(2,1)} %get-tuple-element.18) | copy-start | bytes 393220
  261.8 6.5 %collective-permute-start.2 = (bf16[64,512]{1,0:T(8,128)(2,1)S(1)}, bf16[64,512]{1,0:T(8,128)(2,1)S(1)}, u32[]{:S(2)}, u32[]{:S(2)}) collective-permute-start(bf16[64,512]{1,0:T(8,128)(2,1)S(1)} %convert_element_type.89), channel_id=1, source_target_pairs={{0,2},{2,4},{4,6},{6,8},{8,10},{10,12},{12,14},{14,16},{16,18},{18... | collective-permute-start | bytes 196616 | tf_op jit(solution)/shard_map/ppermute | solution.py:16
  265.2 8.0 %collective-permute-start.3 = (bf16[64,512]{1,0:T(8,128)(2,1)S(1)}, bf16[64,512]{1,0:T(8,128)(2,1)S(1)}, u32[]{:S(2)}, u32[]{:S(2)}) collective-permute-start(bf16[64,512]{1,0:T(8,128)(2,1)S(1)} %convert_element_type.89), channel_id=1, source_target_pairs={{2,0},{4,2},{6,4},{8,6},{10,8},{12,10},{14,12},{16,14},{18,16},{20... | collective-permute-start | bytes 196616 | tf_op jit(solution)/shard_map/ppermute | solution.py:17
Sparse Core Ops, SparseCore 0:
  28.0 80.2 all-gather.7
  111.1 59.4 all-gather.5
  173.9 59.2 all-gather.9
  253.2 7.6 reduce-scatter.1
